TPU v7x, 512 devices: a whole 4x4x16 slice. The times are simulated.
512 devices in a mesh: blk: 128 (over z, y, core), lblk: 4 (over x).
Axes of the slice: x: 4, y: 4, z: 16, core: 2. Of those that a mesh axis runs over, the one named last changes fastest.
Arguments:
- sky: bfloat16 [8, 2, 512, 16384], P(None, None, 'blk', 'lblk'), may hold values from -6 to 6
- arc_start: int32 [2, 512], P(None, 'blk'), may hold values from 0 to 16383
- arc_count: int32 [2, 512], P(None, 'blk'), may hold values from 4096 to 16384
- owner_modes: int32 [512], replicated, may hold values from 0 to 511, each once
- legendre: bfloat16 [512, 128, 4, 4096], P('blk', None, None, 'lblk'), may hold values from -0.25 to 0.25
Outputs:
- alm: float32 [8, 2, 512, 4096], P(None, None, 'blk', 'lblk')
Inputs may be any that keep to these rules, and one draw needn't show every extreme that they name: `owner_modes`: each m-mode 0 to 511 appears exactly once.
All inputs are finite; a program needn't handle non-finite values.
Results may differ from a plain program's by a relative error of at most 0.0049.
Values may be sent and summed in bfloat16 or wider, within the bound.
A program may use at most 64 MiB of HBM per device.

v0:
```python
import math

import jax
import jax.numpy as jnp
from jax import lax
from jax.experimental import pallas as pl
from jax.experimental.pallas import tpu as pltpu
from jax.sharding import PartitionSpec as P

RLEN = 16384
DIFFUSION = 0.2
NX = 4
NZ = 16
NYC = 8
NBLK = NZ * NYC
LANES = 128
G_STRIDE = 40
BF16 = jnp.bfloat16
F32 = jnp.float32


def unit_circle(t):
    t = t & (RLEN - 1)
    q = (t + 2048) >> 12
    theta = (t - (q << 12)).astype(F32) * (2.0 * math.pi / RLEN)
    u = theta * theta
    s = theta * (1.0 + u * (-1.0 / 6 + u * (1.0 / 120 + u * (-1.0 / 5040 + u * (1.0 / 362880)))))
    c = 1.0 + u * (-0.5 + u * (1.0 / 24 + u * (-1.0 / 720 + u * (1.0 / 40320))))
    odd = (q & 1) == 1
    big = jnp.where(odd, s, c)
    small = jnp.where(odd, c, s)
    cos = jnp.where(((q + 1) & 2) == 2, -big, big)
    sin = jnp.where((q & 2) == 2, -small, small)
    return cos, sin


def small_angle(theta):
    u = theta * theta
    s = theta * (1.0 + u * (-1.0 / 6 + u * (1.0 / 120 + u * (-1.0 / 5040))))
    c = 1.0 + u * (-0.5 + u * (1.0 / 24 + u * (-1.0 / 720 + u * (1.0 / 40320))))
    return c, s


def iota(shape, dim):
    return lax.broadcasted_iota(jnp.int32, shape, dim)


def kernel(
    sky_hbm,
    start_ref,
    count_ref,
    modes_s,
    modes_v,
    leg_hbm,
    out_ref,
    sky_v,
    x_ref,
    y_ref,
    modes_ref,
    rs_send,
    rs_recv,
    u_ref,
    z_send,
    z_recv,
    zf_ref,
    g_send,
    g_recv,
    gf_ref,
    leg_raw,
    leg_tmp,
    leg_prep,
    sky_sem,
    leg_sem,
    rs_ssem,
    rs_rsem,
    z_ssem,
    z_rsem,
    g_ssem,
    g_rsem,
):
    blk = lax.axis_index("blk")
    col = lax.axis_index("lblk")
    my_z = blk // NYC
    my_yc = blk % NYC

    sky_copy = pltpu.make_async_copy(sky_hbm, sky_v, sky_sem)
    sky_copy.start()
    leg_copy = pltpu.make_async_copy(leg_hbm, leg_raw, leg_sem)
    leg_copy.start()

    barrier = pltpu.get_barrier_semaphore()

    def greet_z(d, carry):
        pl.semaphore_signal(
            barrier,
            inc=1,
            device_id={"blk": ((my_z + d) % NZ) * NYC + my_yc, "lblk": col},
            device_id_type=pl.DeviceIdType.MESH,
        )
        return carry

    def greet_yx(d, carry):
        pl.semaphore_signal(
            barrier,
            inc=1,
            device_id={
                "blk": my_z * NYC + (my_yc + d // NX) % NYC,
                "lblk": (col + d % NX) % NX,
            },
            device_id_type=pl.DeviceIdType.MESH,
        )
        return carry

    lax.fori_loop(1, NZ, greet_z, 0)
    lax.fori_loop(1, NYC * NX, greet_yx, 0)

    lane8 = iota((8, LANES), 1)
    pick = (4 * (lane8 & 31) + iota((8, LANES), 0)) & (LANES - 1)
    modes = jnp.zeros((8, LANES), jnp.int32)
    for r in range(4):
        row = jnp.broadcast_to(modes_v[r : r + 1, :], (8, LANES))
        got = jnp.take_along_axis(row, pick, axis=1)
        modes = jnp.where((lane8 >> 5) == r, got, modes)
    modes_ref[...] = modes

    sky_copy.wait()
    sub8 = iota((8, LANES), 0)
    k8 = sub8 & 3
    for h in range(2):
        start8 = jnp.zeros((8, LANES), jnp.int32)
        count8 = jnp.zeros((8, LANES), jnp.int32)
        for k in range(4):
            start8 = jnp.where(k8 == k, start_ref[h, k], start8)
            count8 = jnp.where(k8 == k, count_ref[h, k], count8)
        base8 = col * 4096 + (sub8 >> 2) * LANES + lane8 - start8
        keep = [
            ((base8 + 256 * t) & (RLEN - 1)) < count8 for t in range(16)
        ]
        keep = [jnp.where(b, 1.0, 0.0).astype(F32) for b in keep]
        keep_lo = jnp.concatenate(keep[:8], axis=0)
        keep_hi = jnp.concatenate(keep[8:], axis=0)
        for x in range(8):
            r0 = (x * 2 + h) * 128
            lo = sky_v[pl.ds(r0, 64), :].astype(F32)
            hi = sky_v[pl.ds(r0 + 64, 64), :].astype(F32)
            x_ref[pl.ds((x * 2 + h) * 64, 64), 0:128] = (lo * keep_lo).astype(BF16)
            x_ref[pl.ds((x * 2 + h) * 64, 64), 128:256] = (hi * keep_hi).astype(BF16)

    upper = sub8 < 4
    for step, ahead in enumerate((2, 1, 3, 0)):
        chunk = (col + ahead) % NX
        m_row = modes_ref[pl.ds(chunk, 1), :]
        b_index = iota((LANES, LANES), 0)
        lo_c, lo_s = unit_circle(b_index * m_row)
        hi_c, hi_s = unit_circle((b_index + 2048) * m_row)
        table = jnp.concatenate(
            [
                jnp.concatenate([lo_c, -lo_s], axis=1),
                jnp.concatenate([hi_c, -hi_s], axis=1),
            ],
            axis=0,
        ).astype(BF16)
        y_ref[...] = jnp.dot(x_ref[...], table, preferred_element_type=F32)
        lt_index = iota((64, LANES), 0) >> 2
        w_c, w_s = unit_circle((col * 4096 + lt_index * LANES) * m_row)
        w_c = w_c * (1.0 / 128)
        w_s = w_s * (-1.0 / 128)
        for x in range(8):
            acc = []
            for h in range(2):
                re = jnp.zeros((8, LANES), F32)
                im = jnp.zeros((8, LANES), F32)
                for t in range(8):
                    r0 = (x * 2 + h) * 64 + t * 8
                    yc = y_ref[r0 : r0 + 8, 0:128]
                    ys = y_ref[r0 : r0 + 8, 128:256]
                    wc = w_c[t * 8 : t * 8 + 8]
                    ws = w_s[t * 8 : t * 8 + 8]
                    re = re + (yc * wc - ys * ws)
                    im = im + (yc * ws + ys * wc)
                acc.append((re, im))
            for part in range(2):
                plus = acc[0][part] + acc[1][part]
                minus = acc[0][part] - acc[1][part]
                plus = plus + pltpu.roll(plus, 4, axis=0)
                minus = minus + pltpu.roll(minus, 4, axis=0)
                r0 = part * 64 + x * 8
                u_ref[r0 : r0 + 8, :] = jnp.where(upper, plus, minus)
        if ahead == 0:
            break
        rs_send[step] = u_ref[...].astype(BF16)
        if step == 0:
            pl.semaphore_wait(barrier, NZ - 1 + NYC * NX - 1)
        pltpu.make_async_remote_copy(
            src_ref=rs_send.at[step],
            dst_ref=rs_recv.at[step],
            send_sem=rs_ssem.at[step],
            recv_sem=rs_rsem.at[step],
            device_id={"blk": blk, "lblk": chunk},
            device_id_type=pl.DeviceIdType.MESH,
        ).start()

    def prepare(s):
        def group(gb, carry):
            raw = leg_raw[s, pl.ds(gb * 512, 512), :].astype(F32)
            for g in range(16):
                leg_tmp[g * G_STRIDE : g * G_STRIDE + 32, :] = raw[g * 32 : g * 32 + 32]
            for lt in range(8):
                for r in range(4):
                    rows = leg_tmp[pl.ds(lt * 4 + r, 16, stride=G_STRIDE), :]
                    leg_prep[s, pl.ds(r * 128 + gb * 16, 16), lt * 128 : lt * 128 + 128] = (
                        rows.astype(BF16)
                    )
            return carry

        lax.fori_loop(0, 8, group, 0)

    leg_copy.wait()
    prepare(0)

    def rs_copy(step):
        return pltpu.make_async_remote_copy(
            src_ref=rs_send.at[step],
            dst_ref=rs_recv.at[step],
            send_sem=rs_ssem.at[step],
            recv_sem=rs_rsem.at[step],
            device_id={"blk": blk, "lblk": (col + 1) % NX},
            device_id_type=pl.DeviceIdType.MESH,
        )

    total = u_ref[...]
    for step in range(3):
        rs_copy(step).wait_recv()
    for step in range(3):
        total = total + rs_recv[step].astype(F32)
    u_ref[...] = total

    ordered = jnp.concatenate(
        [
            u_ref[pl.ds(part * 64 + sign * 4 + k, 8, stride=8), :]
            for k in range(4)
            for part in range(2)
            for sign in range(2)
        ],
        axis=0,
    )
    turned = ordered.T
    for z in range(NZ):
        z_send[z] = turned[z * 8 : z * 8 + 8].astype(BF16)

    def z_copy(d):
        return pltpu.make_async_remote_copy(
            src_ref=z_send.at[(my_z + d) % NZ],
            dst_ref=z_recv.at[my_z],
            send_sem=z_ssem.at[d],
            recv_sem=z_rsem.at[d],
            device_id={"blk": ((my_z + d) % NZ) * NYC + my_yc, "lblk": col},
            device_id_type=pl.DeviceIdType.MESH,
        )

    for d in (8, 7, 9, 6, 10, 5, 11, 4, 12, 3, 13, 2, 14, 1, 15):
        z_copy(d).start()
    z_recv[my_z] = z_send[my_z]
    prepare(1)
    prepare(2)
    prepare(3)

    def z_wait(d, carry):
        z_copy(d).wait_recv()
        return carry

    lax.fori_loop(1, NZ, z_wait, 0)
    for z in range(NZ):
        zf_ref[z * 8 : z * 8 + 8, :] = z_recv[z].astype(F32)
    for yc in range(NYC):
        g_send[yc] = zf_ref[pl.ds(yc, NZ, stride=8), :].astype(BF16)

    def g_copy(d):
        yc = (my_yc + d // NX) % NYC
        return pltpu.make_async_remote_copy(
            src_ref=g_send.at[yc],
            dst_ref=g_recv.at[col, my_yc],
            send_sem=g_ssem.at[d],
            recv_sem=g_rsem.at[d],
            device_id={"blk": my_z * NYC + yc, "lblk": (col + d % NX) % NX},
            device_id_type=pl.DeviceIdType.MESH,
        )

    for dx in (0, 2, 1, 3):
        for dyc in (4, 5, 3, 2, 6, 7, 1, 0):
            if dx or dyc:
                g_copy(dyc * NX + dx).start()
    g_recv[col, my_yc] = g_send[my_yc]

    lane_row = iota((8, LANES), 1)
    degree = iota((8, 1024), 1) + col * 1024
    for ahead in (0, 1, 3, 2):
        source = (col + NX - ahead) % NX

        def g_wait(j, carry, ahead=ahead):
            g_copy(j * NX + ahead).wait_recv()
            return carry

        lax.fori_loop(1 if ahead == 0 else 0, NYC, g_wait, 0)
        for yc in range(NYC):
            gf_ref[yc * NZ : yc * NZ + NZ, :] = g_recv[source, yc].astype(F32)
        by_cycle = jnp.concatenate(
            [gf_ref[pl.ds(z, NYC, stride=NZ), :] for z in range(NZ)], axis=0
        )
        turned = by_cycle.T
        mode = modes_s[blk * NX + source]
        theta = jnp.full((8, LANES), mode, jnp.int32).astype(F32) * (math.pi / RLEN)
        turn_c, turn_s = small_angle(theta)
        double_c, _ = small_angle(theta * 2.0)
        centre = (1.0 - 4.0 * DIFFUSION) + 2.0 * DIFFUSION * double_c
        rows = {}
        for sign in range(2):
            smooth = {}
            for part in range(2):
                a = [
                    turned[(k * 4 + part * 2 + sign) * 8 : (k * 4 + part * 2 + sign) * 8 + 8]
                    for k in range(4)
                ]
                above = jnp.where(lane_row == 0, 0.0, pltpu.roll(a[3], 1, axis=1))
                edge = a[3] if sign == 0 else -a[3]
                below = jnp.where(
                    lane_row == LANES - 1, edge, pltpu.roll(a[0], LANES - 1, axis=1)
                )
                full = [above] + a + [below]
                for k in range(4):
                    smooth[part, k] = centre * a[k] + DIFFUSION * (full[k] + full[k + 2])
            for k in range(4):
                re, im = smooth[0, k], smooth[1, k]
                if k % 2:
                    re, im = re * turn_c + im * turn_s, im * turn_c - re * turn_s
                rows[sign, 0, k] = re
                rows[sign, 1, k] = im
        lhs = jnp.concatenate(
            [
                jnp.concatenate(
                    [rows[sign, part, k] for sign in range(2) for part in range(2)], axis=0
                )
                for k in range(4)
            ],
            axis=1,
        ).astype(BF16)
        sums = jnp.dot(lhs, leg_prep[source], preferred_element_type=F32)
        even = ((degree + mode) & 1) == 0
        inside = degree >= mode
        for part in range(2):
            chosen = jnp.where(
                even, sums[part * 8 : part * 8 + 8], sums[16 + part * 8 : 24 + part * 8]
            )
            chosen = jnp.where(inside, chosen, 0.0)
            for lt in range(8):
                out_ref[pl.ds(part * 32 + lt * 4 + source, 8, stride=64), :] = chosen[
                    :, lt * 128 : lt * 128 + 128
                ]

    for step in range(3):
        rs_copy(step).wait_send()

    def z_done(d, carry):
        z_copy(d).wait_send()
        return carry

    def g_done(d, carry):
        g_copy(d).wait_send()
        return carry

    lax.fori_loop(1, NZ, z_done, 0)
    lax.fori_loop(1, NYC * NX, g_done, 0)


def local(sky, arc_start, arc_count, owner_modes, legendre):
    sky_rows = sky.reshape(16, 4, 32, 128).transpose(0, 2, 1, 3).reshape(2048, 128)
    leg_rows = (
        legendre.reshape(4, 128, 4, 8, 128).transpose(0, 1, 3, 2, 4).reshape(4, 4096, 128)
    )
    any_space = pl.BlockSpec(memory_space=pl.ANY)
    vmem = pl.BlockSpec(memory_space=pltpu.VMEM)
    smem = pl.BlockSpec(memory_space=pltpu.SMEM)
    out = pl.pallas_call(
        kernel,
        out_shape=jax.ShapeDtypeStruct((512, 128), F32),
        in_specs=[any_space, smem, smem, smem, vmem, any_space],
        out_specs=vmem,
        scratch_shapes=[
            pltpu.VMEM((2048, 128), BF16),
            pltpu.VMEM((1024, 256), BF16),
            pltpu.VMEM((1024, 256), F32),
            pltpu.VMEM((8, 128), jnp.int32),
            pltpu.VMEM((3, 128, 128), BF16),
            pltpu.VMEM((3, 128, 128), BF16),
            pltpu.VMEM((128, 128), F32),
            pltpu.VMEM((NZ, 8, 128), BF16),
            pltpu.VMEM((NZ, 8, 128), BF16),
            pltpu.VMEM((128, 128), F32),
            pltpu.VMEM((NYC, NZ, 128), BF16),
            pltpu.VMEM((NX, NYC, NZ, 128), BF16),
            pltpu.VMEM((128, 128), F32),
            pltpu.VMEM((4, 4096, 128), BF16),
            pltpu.VMEM((16 * G_STRIDE, 128), F32),
            pltpu.VMEM((4, 512, 1024), BF16),
            pltpu.SemaphoreType.DMA,
            pltpu.SemaphoreType.DMA,
            pltpu.SemaphoreType.DMA((3,)),
            pltpu.SemaphoreType.DMA((3,)),
            pltpu.SemaphoreType.DMA((NZ,)),
            pltpu.SemaphoreType.DMA((NZ,)),
            pltpu.SemaphoreType.DMA((NYC * NX,)),
            pltpu.SemaphoreType.DMA((NYC * NX,)),
        ],
        compiler_params=pltpu.CompilerParams(
            collective_id=0, has_side_effects=True, vmem_limit_bytes=67043328
        ),
    )(sky_rows, arc_start, arc_count, owner_modes, owner_modes.reshape(4, 128), leg_rows)
    return out.reshape(8, 2, 8, 4, 128).transpose(0, 1, 3, 2, 4).reshape(8, 2, 4, 1024)


def solution(mesh):
    return jax.shard_map(
        local,
        mesh=mesh,
        in_specs=(
            P(None, None, "blk", "lblk"),
            P(None, "blk"),
            P(None, "blk"),
            P(),
            P("blk", None, None, "lblk"),
        ),
        out_specs=P(None, None, "blk", "lblk"),
        check_vma=False,
    )
```

profile of v0, /device:TPU:1, one launch (start us, length us, event | category | flops | bytes accessed | tf_op | source)
XLA Modules:
  0.0 38.5 jit_solution(10392336362949487139)
XLA Ops:
  0.0 36.8 %shard_map.55 = f32[512,128]{1,0:T(8,128)} custom-call(bf16[2048,128]{1,0:T(8,128)(2,1)} %bitcast.18, s32[2,4]{1,0:T(2,128)} %start_ref.1, s32[2,4]{1,0:T(2,128)} %count_ref.1, s32[512]{0:T(512)} %modes_s.1, s32[4,128]{1,0:T(4,128)} %bitcast.19, bf16[4,4096,128]{2,1,0:T(8,128)(2,1)} %bitcast.16), custom_call_target="tpu_custom_call" | custom-call | tf_op jit(solution)/shard_map/pallas_call | solution.py:383
  36.8 1.7 %copy.10 = f32[8,2,4,1024]{3,2,1,0:T(4,128)} copy(f32[8,2,4,1024]{3,2,1,0:T(4,128)} %bitcast.17) | data formatting | bytes 524288
where the time goes:
time: 38.6 us; the launch traced here: 38.5 us
  Pallas kernels  36.8 us (95%)
  local copies, waits for them, and re-layouts  1.67 us (4%)
    pallas_call x1, Pallas kernels, local(): pl.pallas_call(kernel, out_shape=jax.ShapeDtypeStruct((512, 128), F32), i...  36.8 us
    unnamed x1, local copies, waits for them, and re-layouts  1.67 us

commit v1 on v0

--- a/solution.py
+++ b/solution.py
@@ -47,15 +47,20 @@
 
 def kernel(
     sky_hbm,
+    start_hbm,
+    count_hbm,
+    modes_hbm,
+    leg_hbm,
+    out_ref,
     start_ref,
     count_ref,
     modes_s,
     modes_v,
-    leg_hbm,
-    out_ref,
     sky_v,
     x_ref,
     y_ref,
+    table_ref,
+    turn_ref,
     modes_ref,
     rs_send,
     rs_recv,
@@ -71,6 +76,7 @@
     leg_prep,
     sky_sem,
     leg_sem,
+    small_sem,
     rs_ssem,
     rs_rsem,
     z_ssem,
@@ -80,40 +86,41 @@
 ):
     blk = lax.axis_index("blk")
     col = lax.axis_index("lblk")
-    my_z = blk // NYC
-    my_yc = blk % NYC
-
+    my_z = blk >> 3
+    my_yc = blk & 7
+
+    barrier = pltpu.get_barrier_semaphore()
+
+    def place(z, yc, x):
+        return {"blk": ((z & 15) << 3) | (yc & 7), "lblk": x & 3}
+
+    def greet(target):
+        pl.semaphore_signal(
+            barrier, inc=1, device_id=target, device_id_type=pl.DeviceIdType.MESH
+        )
+
+    small = [
+        pltpu.make_async_copy(modes_hbm, modes_v, small_sem.at[0]),
+        pltpu.make_async_copy(start_hbm, start_ref, small_sem.at[1]),
+        pltpu.make_async_copy(count_hbm, count_ref, small_sem.at[2]),
+        pltpu.make_async_copy(modes_hbm, modes_s, small_sem.at[3]),
+    ]
     sky_copy = pltpu.make_async_copy(sky_hbm, sky_v, sky_sem)
+    leg_copy = pltpu.make_async_copy(leg_hbm, leg_raw, leg_sem)
+    for copy in small[:3]:
+        copy.start()
     sky_copy.start()
-    leg_copy = pltpu.make_async_copy(leg_hbm, leg_raw, leg_sem)
+    small[3].start()
     leg_copy.start()
-
-    barrier = pltpu.get_barrier_semaphore()
-
-    def greet_z(d, carry):
-        pl.semaphore_signal(
-            barrier,
-            inc=1,
-            device_id={"blk": ((my_z + d) % NZ) * NYC + my_yc, "lblk": col},
-            device_id_type=pl.DeviceIdType.MESH,
-        )
-        return carry
-
-    def greet_yx(d, carry):
-        pl.semaphore_signal(
-            barrier,
-            inc=1,
-            device_id={
-                "blk": my_z * NYC + (my_yc + d // NX) % NYC,
-                "lblk": (col + d % NX) % NX,
-            },
-            device_id_type=pl.DeviceIdType.MESH,
-        )
-        return carry
-
-    lax.fori_loop(1, NZ, greet_z, 0)
-    lax.fori_loop(1, NYC * NX, greet_yx, 0)
-
+    for dx in (2, 1, 3):
+        greet(place(my_z, my_yc, col + dx))
+    for dz in (8, 7, 9, 6, 10, 5, 11, 4, 12, 3, 13, 2, 14, 1, 15):
+        greet(place(my_z + dz, my_yc, col))
+    for dyc in range(1, 8):
+        for dx in range(4):
+            greet(place(my_z, my_yc + dyc, col + dx))
+
+    small[0].wait()
     lane8 = iota((8, LANES), 1)
     pick = (4 * (lane8 & 31) + iota((8, LANES), 0)) & (LANES - 1)
     modes = jnp.zeros((8, LANES), jnp.int32)
@@ -123,6 +130,21 @@
         modes = jnp.where((lane8 >> 5) == r, got, modes)
     modes_ref[...] = modes
 
+    steps = (2, 1, 3, 0)
+    b_index = iota((LANES, LANES), 0)
+    lt_index = iota((64, LANES), 0) >> 2
+    for step, ahead in enumerate(steps):
+        m_row = modes_ref[pl.ds((col + ahead) & 3, 1), :]
+        for hi in range(2):
+            c, sn = unit_circle((b_index + 2048 * hi) * m_row)
+            table_ref[step, hi * 128 : hi * 128 + 128, 0:128] = c.astype(BF16)
+            table_ref[step, hi * 128 : hi * 128 + 128, 128:256] = (-sn).astype(BF16)
+        c, sn = unit_circle((col * 4096 + lt_index * LANES) * m_row)
+        turn_ref[step, 0] = c * (1.0 / 128)
+        turn_ref[step, 1] = sn * (-1.0 / 128)
+
+    small[1].wait()
+    small[2].wait()
     sky_copy.wait()
     sub8 = iota((8, LANES), 0)
     k8 = sub8 & 3
@@ -147,24 +169,11 @@
             x_ref[pl.ds((x * 2 + h) * 64, 64), 128:256] = (hi * keep_hi).astype(BF16)
 
     upper = sub8 < 4
-    for step, ahead in enumerate((2, 1, 3, 0)):
-        chunk = (col + ahead) % NX
-        m_row = modes_ref[pl.ds(chunk, 1), :]
-        b_index = iota((LANES, LANES), 0)
-        lo_c, lo_s = unit_circle(b_index * m_row)
-        hi_c, hi_s = unit_circle((b_index + 2048) * m_row)
-        table = jnp.concatenate(
-            [
-                jnp.concatenate([lo_c, -lo_s], axis=1),
-                jnp.concatenate([hi_c, -hi_s], axis=1),
-            ],
-            axis=0,
-        ).astype(BF16)
-        y_ref[...] = jnp.dot(x_ref[...], table, preferred_element_type=F32)
-        lt_index = iota((64, LANES), 0) >> 2
-        w_c, w_s = unit_circle((col * 4096 + lt_index * LANES) * m_row)
-        w_c = w_c * (1.0 / 128)
-        w_s = w_s * (-1.0 / 128)
+    for step, ahead in enumerate(steps):
+        chunk = (col + ahead) & 3
+        y_ref[step] = jnp.dot(x_ref[...], table_ref[step], preferred_element_type=F32)
+        w_c = turn_ref[step, 0]
+        w_s = turn_ref[step, 1]
         for x in range(8):
             acc = []
             for h in range(2):
@@ -172,8 +181,8 @@
                 im = jnp.zeros((8, LANES), F32)
                 for t in range(8):
                     r0 = (x * 2 + h) * 64 + t * 8
-                    yc = y_ref[r0 : r0 + 8, 0:128]
-                    ys = y_ref[r0 : r0 + 8, 128:256]
+                    yc = y_ref[step, r0 : r0 + 8, 0:128]
+                    ys = y_ref[step, r0 : r0 + 8, 128:256]
                     wc = w_c[t * 8 : t * 8 + 8]
                     ws = w_s[t * 8 : t * 8 + 8]
                     re = re + (yc * wc - ys * ws)
@@ -224,13 +233,13 @@
             dst_ref=rs_recv.at[step],
             send_sem=rs_ssem.at[step],
             recv_sem=rs_rsem.at[step],
-            device_id={"blk": blk, "lblk": (col + 1) % NX},
+            device_id={"blk": blk, "lblk": (col + 1) & 3},
             device_id_type=pl.DeviceIdType.MESH,
         )
 
     total = u_ref[...]
     for step in range(3):
-        rs_copy(step).wait_recv()
+        rs_copy(step).wait()
     for step in range(3):
         total = total + rs_recv[step].astype(F32)
     u_ref[...] = total
@@ -248,67 +257,68 @@
     for z in range(NZ):
         z_send[z] = turned[z * 8 : z * 8 + 8].astype(BF16)
 
-    def z_copy(d):
-        return pltpu.make_async_remote_copy(
-            src_ref=z_send.at[(my_z + d) % NZ],
+    for d in (8, 7, 9, 6, 10, 5, 11, 4, 12, 3, 13, 2, 14, 1, 15):
+        pltpu.make_async_remote_copy(
+            src_ref=z_send.at[(my_z + d) & 15],
             dst_ref=z_recv.at[my_z],
-            send_sem=z_ssem.at[d],
-            recv_sem=z_rsem.at[d],
-            device_id={"blk": ((my_z + d) % NZ) * NYC + my_yc, "lblk": col},
+            send_sem=z_ssem,
+            recv_sem=z_rsem,
+            device_id=place(my_z + d, my_yc, col),
             device_id_type=pl.DeviceIdType.MESH,
-        )
-
-    for d in (8, 7, 9, 6, 10, 5, 11, 4, 12, 3, 13, 2, 14, 1, 15):
-        z_copy(d).start()
+        ).start()
     z_recv[my_z] = z_send[my_z]
     prepare(1)
     prepare(2)
     prepare(3)
-
-    def z_wait(d, carry):
-        z_copy(d).wait_recv()
-        return carry
-
-    lax.fori_loop(1, NZ, z_wait, 0)
+    small[3].wait()
+    others = pl.ds(0, NZ - 1)
+    pltpu.make_async_remote_copy(
+        src_ref=z_send.at[others],
+        dst_ref=z_recv.at[others],
+        send_sem=z_ssem,
+        recv_sem=z_rsem,
+        device_id=place(my_z + 1, my_yc, col),
+        device_id_type=pl.DeviceIdType.MESH,
+    ).wait()
     for z in range(NZ):
         zf_ref[z * 8 : z * 8 + 8, :] = z_recv[z].astype(F32)
     for yc in range(NYC):
         g_send[yc] = zf_ref[pl.ds(yc, NZ, stride=8), :].astype(BF16)
 
-    def g_copy(d):
-        yc = (my_yc + d // NX) % NYC
-        return pltpu.make_async_remote_copy(
-            src_ref=g_send.at[yc],
-            dst_ref=g_recv.at[col, my_yc],
-            send_sem=g_ssem.at[d],
-            recv_sem=g_rsem.at[d],
-            device_id={"blk": my_z * NYC + yc, "lblk": (col + d % NX) % NX},
-            device_id_type=pl.DeviceIdType.MESH,
-        )
-
-    for dx in (0, 2, 1, 3):
+    for dx in (2, 1, 3, 0):
         for dyc in (4, 5, 3, 2, 6, 7, 1, 0):
             if dx or dyc:
-                g_copy(dyc * NX + dx).start()
+                pltpu.make_async_remote_copy(
+                    src_ref=g_send.at[(my_yc + dyc) & 7],
+                    dst_ref=g_recv.at[col, my_yc],
+                    send_sem=g_ssem.at[dx],
+                    recv_sem=g_rsem.at[dx],
+                    device_id=place(my_z, my_yc + dyc, col + dx),
+                    device_id_type=pl.DeviceIdType.MESH,
+                ).start()
     g_recv[col, my_yc] = g_send[my_yc]
 
     lane_row = iota((8, LANES), 1)
     degree = iota((8, 1024), 1) + col * 1024
-    for ahead in (0, 1, 3, 2):
-        source = (col + NX - ahead) % NX
-
-        def g_wait(j, carry, ahead=ahead):
-            g_copy(j * NX + ahead).wait_recv()
-            return carry
-
-        lax.fori_loop(1 if ahead == 0 else 0, NYC, g_wait, 0)
+    for dx in range(NX):
+        group = pl.ds(0, NYC - 1 if dx == 0 else NYC)
+        pltpu.make_async_remote_copy(
+            src_ref=g_send.at[group],
+            dst_ref=g_recv.at[(col - dx) & 3, group],
+            send_sem=g_ssem.at[dx],
+            recv_sem=g_rsem.at[dx],
+            device_id=place(my_z, my_yc + 1, col),
+            device_id_type=pl.DeviceIdType.MESH,
+        ).wait()
+    for ahead in range(NX):
+        source = (col - ahead) & 3
         for yc in range(NYC):
-            gf_ref[yc * NZ : yc * NZ + NZ, :] = g_recv[source, yc].astype(F32)
+            gf_ref[ahead, yc * NZ : yc * NZ + NZ, :] = g_recv[source, yc].astype(F32)
         by_cycle = jnp.concatenate(
-            [gf_ref[pl.ds(z, NYC, stride=NZ), :] for z in range(NZ)], axis=0
+            [gf_ref[ahead, pl.ds(z, NYC, stride=NZ), :] for z in range(NZ)], axis=0
         )
         turned = by_cycle.T
-        mode = modes_s[blk * NX + source]
+        mode = modes_s[blk >> 5, ((blk & 31) << 2) | source]
         theta = jnp.full((8, LANES), mode, jnp.int32).astype(F32) * (math.pi / RLEN)
         turn_c, turn_s = small_angle(theta)
         double_c, _ = small_angle(theta * 2.0)
@@ -357,38 +367,29 @@
                     :, lt * 128 : lt * 128 + 128
                 ]
 
-    for step in range(3):
-        rs_copy(step).wait_send()
-
-    def z_done(d, carry):
-        z_copy(d).wait_send()
-        return carry
-
-    def g_done(d, carry):
-        g_copy(d).wait_send()
-        return carry
-
-    lax.fori_loop(1, NZ, z_done, 0)
-    lax.fori_loop(1, NYC * NX, g_done, 0)
-
 
 def local(sky, arc_start, arc_count, owner_modes, legendre):
     sky_rows = sky.reshape(16, 4, 32, 128).transpose(0, 2, 1, 3).reshape(2048, 128)
     leg_rows = (
         legendre.reshape(4, 128, 4, 8, 128).transpose(0, 1, 3, 2, 4).reshape(4, 4096, 128)
     )
-    any_space = pl.BlockSpec(memory_space=pl.ANY)
-    vmem = pl.BlockSpec(memory_space=pltpu.VMEM)
-    smem = pl.BlockSpec(memory_space=pltpu.SMEM)
+    operands = [sky_rows, arc_start, arc_count, owner_modes.reshape(4, 128), leg_rows]
+    operands = [pltpu.with_memory_space_constraint(a, pltpu.HBM) for a in operands]
     out = pl.pallas_call(
         kernel,
-        out_shape=jax.ShapeDtypeStruct((512, 128), F32),
-        in_specs=[any_space, smem, smem, smem, vmem, any_space],
-        out_specs=vmem,
+        out_shape=pltpu.VMEM((512, 128), F32),
+        in_specs=[pl.BlockSpec(memory_space=pltpu.HBM)] * 5,
+        out_specs=pl.BlockSpec(memory_space=pltpu.VMEM),
         scratch_shapes=[
+            pltpu.SMEM((2, 4), jnp.int32),
+            pltpu.SMEM((2, 4), jnp.int32),
+            pltpu.SMEM((4, 128), jnp.int32),
+            pltpu.VMEM((4, 128), jnp.int32),
             pltpu.VMEM((2048, 128), BF16),
             pltpu.VMEM((1024, 256), BF16),
-            pltpu.VMEM((1024, 256), F32),
+            pltpu.VMEM((4, 1024, 256), F32),
+            pltpu.VMEM((4, 256, 256), BF16),
+            pltpu.VMEM((4, 2, 64, 128), F32),
             pltpu.VMEM((8, 128), jnp.int32),
             pltpu.VMEM((3, 128, 128), BF16),
             pltpu.VMEM((3, 128, 128), BF16),
@@ -398,23 +399,24 @@
             pltpu.VMEM((128, 128), F32),
             pltpu.VMEM((NYC, NZ, 128), BF16),
             pltpu.VMEM((NX, NYC, NZ, 128), BF16),
-            pltpu.VMEM((128, 128), F32),
+            pltpu.VMEM((4, 128, 128), F32),
             pltpu.VMEM((4, 4096, 128), BF16),
             pltpu.VMEM((16 * G_STRIDE, 128), F32),
             pltpu.VMEM((4, 512, 1024), BF16),
             pltpu.SemaphoreType.DMA,
             pltpu.SemaphoreType.DMA,
+            pltpu.SemaphoreType.DMA((4,)),
             pltpu.SemaphoreType.DMA((3,)),
             pltpu.SemaphoreType.DMA((3,)),
-            pltpu.SemaphoreType.DMA((NZ,)),
-            pltpu.SemaphoreType.DMA((NZ,)),
-            pltpu.SemaphoreType.DMA((NYC * NX,)),
-            pltpu.SemaphoreType.DMA((NYC * NX,)),
+            pltpu.SemaphoreType.DMA,
+            pltpu.SemaphoreType.DMA,
+            pltpu.SemaphoreType.DMA((NX,)),
+            pltpu.SemaphoreType.DMA((NX,)),
         ],
         compiler_params=pltpu.CompilerParams(
-            collective_id=0, has_side_effects=True, vmem_limit_bytes=67043328
+            collective_id=0, has_side_effects=True, vmem_limit_bytes=48 * 1024 * 1024
         ),
-    )(sky_rows, arc_start, arc_count, owner_modes, owner_modes.reshape(4, 128), leg_rows)
+    )(*operands)
     return out.reshape(8, 2, 8, 4, 128).transpose(0, 1, 3, 2, 4).reshape(8, 2, 4, 1024)
 
 

time: 38.6 us -> 34.4 us (0.89)
  Pallas kernels: 36.8 us -> 33.6 us
  local copies, waits for them, and re-layouts: 1.67 us -> 0.71 us
    pallas_call x1, Pallas kernels: 36.8 us -> 33.6 us  [local(): pl.pallas_call(kernel, out_shape=pltpu.VMEM((512, 128), F32), in_specs=[p...]
    unnamed x1, local copies, waits for them, and re-layouts: 1.67 us -> 0.71 us
where the time goes in v1:
time: 34.4 us; the launch traced here: 34.3 us
  Pallas kernels  33.6 us (98%)
  local copies, waits for them, and re-layouts  0.71 us (2%)
    pallas_call x1, Pallas kernels, local(): pl.pallas_call(kernel, out_shape=pltpu.VMEM((512, 128), F32), in_specs=[p...  33.6 us
    unnamed x1, local copies, waits for them, and re-layouts  0.71 us

profile of v1, /device:TPU:1, one launch (start us, length us, event | category | flops | bytes accessed | tf_op | source)
XLA Modules:
  0.0 34.3 jit_solution(10796016779986134999)
XLA Ops:
  0.0 33.6 %shard_map.55 = f32[512,128]{1,0:T(8,128)S(1)} custom-call(bf16[2048,128]{1,0:T(8,128)(2,1)} %bitcast.18, s32[2,4]{1,0:T(2,128)} %start_hbm.1, s32[2,4]{1,0:T(2,128)} %count_hbm.1, s32[4,128]{1,0:T(4,128)} %bitcast.19, bf16[4,4096,128]{2,1,0:T(8,128)(2,1)} %bitcast.17), custom_call_target="tpu_custom_call" | custom-call | tf_op jit(solution)/shard_map/pallas_call | solution.py:378
  33.6 0.7 %copy.10 = f32[8,2,4,1024]{3,2,1,0:T(4,128)} copy(f32[8,2,4,1024]{3,2,1,0:T(4,128)S(1)} %bitcast.16) | data formatting | bytes 524288
